TPU v7x, 256 devices: a whole 4x4x8 slice. The times are simulated.
256 devices in a mesh: bank: 16 (over z, core), zero: 16 (over y, x).
Axes of the slice: x: 4, y: 4, z: 8, core: 2. Of those that a mesh axis runs over, the one named last changes fastest.
Arguments:
- master_gate: float32 [64, 2048, 1408], P('bank', 'zero'), may hold values from -0.1875 to 0.1875
- master_up: float32 [64, 2048, 1408], P('bank', 'zero'), may hold values from -0.1875 to 0.1875
- master_down: float32 [64, 1408, 2048], P('bank', None, 'zero'), may hold values from -0.21875 to 0.21875
- router_weight: float32 [2048, 64], P('zero', 'bank'), may hold values from -0.125 to 0.125
- router_gain: float32 [2048], P('zero'), may hold values from 0.25 to 1.75
Outputs:
- final_gate: bfloat16 [64, 2048, 1408], P('bank', None, 'zero')
- final_up: bfloat16 [64, 2048, 1408], P('bank', None, 'zero')
- final_down: bfloat16 [64, 1408, 2048], P('bank', 'zero')
- scale_gate: float32 [64, 1408], P('bank', 'zero')
- scale_up: float32 [64, 1408], P('bank', 'zero')
- scale_down: float32 [64, 1408], P('bank', 'zero')
- serve_router: bfloat16 [2048, 64], replicated
All inputs are finite; a program needn't handle non-finite values. Where the computation divides by a largest or mean magnitude, that divisor is 1e-20 or more.
Results may differ from a plain program's by a relative error of at most 0.0013.
Values may be sent and summed in bfloat16 or wider, within the bound.
A program may use at most 64 MiB of HBM per device.

v0:
```python
import jax
import jax.numpy as jnp
from jax import lax
from jax.sharding import PartitionSpec as P

D_MODEL = 2048


def copy_for_each(x, axis):
    count = lax.axis_size(axis)
    return lax.all_to_all(jnp.broadcast_to(x[None], (count, *x.shape)), axis, 0, 0, tiled=True)


def taken_together(x, axis):
    return copy_for_each(x, axis).sum(axis=0)


def in_one(arrays, axis):
    vector, at, finished = (jnp.concatenate([a.reshape(-1) for a in arrays]), 0, [])
    total = taken_together(vector, axis)
    for a in arrays:
        finished.append(total[at : at + a.size].reshape(a.shape))
        at += a.size
    return tuple(finished)


def side_by_side(arrays, axis, split_dim, concat_dim, along):
    both = jnp.concatenate(arrays, axis=along)
    whole, at, finished = (
        lax.all_to_all(both, axis, split_axis=split_dim, concat_axis=concat_dim, tiled=True),
        0,
        [],
    )
    for a in arrays:
        finished.append(lax.slice_in_dim(whole, at, at + a.shape[along], axis=along))
        at += a.shape[along]
    return tuple(finished)


def laid_out(pieces, dim):
    shape = list(pieces.shape[1:])
    shape[dim] *= pieces.shape[0]
    return jnp.moveaxis(pieces, 0, dim).reshape(shape)


def gather_directly(x, axis, dim):
    pieces = copy_for_each(x, axis)
    return laid_out(pieces, dim)


def local(master_gate, master_up, master_down, router_weight, router_gain):
    total_gate, total_up, total_down = in_one(
        (
            jnp.sum(jnp.abs(master_gate), axis=1),
            jnp.sum(jnp.abs(master_up), axis=1),
            jnp.sum(jnp.abs(master_down), axis=2),
        ),
        "zero",
    )
    scale_gate = total_gate / D_MODEL
    scale_up = total_up / D_MODEL
    scale_down = total_down / D_MODEL
    narrow_gate, narrow_up, narrow_down = (
        (master_gate / jnp.expand_dims(scale_gate, 1)).astype(jnp.bfloat16),
        (master_up / jnp.expand_dims(scale_up, 1)).astype(jnp.bfloat16),
        (master_down / jnp.expand_dims(scale_down, 2)).astype(jnp.bfloat16),
    )
    final_gate, final_up = side_by_side((narrow_gate, narrow_up), "zero", 2, 1, 0)
    final_down = lax.all_to_all(narrow_down, "zero", split_axis=1, concat_axis=2, tiled=True)
    scale_gate = lax.dynamic_slice_in_dim(
        scale_gate, lax.axis_index("zero") * final_gate.shape[2], final_gate.shape[2], axis=1
    )
    scale_up = lax.dynamic_slice_in_dim(
        scale_up, lax.axis_index("zero") * final_up.shape[2], final_up.shape[2], axis=1
    )
    scale_down = lax.dynamic_slice_in_dim(
        scale_down, lax.axis_index("zero") * final_down.shape[1], final_down.shape[1], axis=1
    )
    part_router = (router_weight * router_gain[:, None]).astype(jnp.bfloat16)
    row_router = gather_directly(part_router, "zero", 0)
    serve_router = lax.all_gather(row_router, "bank", axis=1, tiled=True)
    return (final_gate, final_up, final_down, scale_gate, scale_up, scale_down, serve_router)


def solution(mesh):
    placed = (
        P("bank", "zero", None),
        P("bank", "zero", None),
        P("bank", None, "zero"),
        P("zero", "bank"),
        P("zero"),
    )
    return jax.shard_map(
        local,
        mesh=mesh,
        in_specs=placed,
        out_specs=(
            P("bank", None, "zero"),
            P("bank", None, "zero"),
            P("bank", "zero", None),
            P("bank", "zero"),
            P("bank", "zero"),
            P("bank", "zero"),
            P(),
        ),
        check_vma=False,
    )
```

profile of v0, /device:TPU:224, one launch (start us, length us, event | category | flops | bytes accessed | tf_op | source)
XLA Modules:
  0.0 125.6 jit_solution(8950060846199024515)
XLA Ops:
  0.6 0.0 copy-start.1
  0.6 2.2 %abs_reduce_fusion.2 = f32[4,1408]{1,0:T(4,128)S(1)} fusion(f32[4,128,1408]{2,1,0:T(8,128)} %param.5), kind=kLoop, calls=%fused_computation.4 | loop fusion | flops 1436160 | bytes 2906112 | tf_op jit(solution)/shard_map/reduce_sum | solution.py:54
  2.9 0.4 copy-done.1
  3.3 0.2 abs_reduce_fusion.1
  3.6 0.0 copy-start
  3.6 2.8 %abs_reduce_fusion = f32[4,1408]{1,0:T(4,128)S(1)} fusion(f32[4,1408,128]{2,1,0:T(8,128)} %param.7), kind=kLoop, calls=%fused_computation.2 | loop fusion | flops 1436160 | bytes 2906112 | tf_op jit(solution)/shard_map/reduce_sum | solution.py:56
  6.4 1.5 %broadcast_in_dim.4 = f32[16,1,16896]{2,1,0:T(1,128)} broadcast(f32[16896]{0:T(1024)S(1)} %pad_maximum_fusion.1), dimensions={2} | broadcast | bytes 1148928 | tf_op jit(solution)/shard_map/broadcast_in_dim | solution.py:11
  8.0 7.1 %all-to-all-start = ((f32[16,1,16896]{2,1,0:T(1,128)}), f32[16,1,16896]{2,1,0:T(1,128)}, u32[]{:S(2)}, u32[]{:S(2)}) async-start(f32[16,1,16896]{2,1,0:T(1,128)} %broadcast_in_dim.4), calls=%async_computation | async-start | bytes 2162688 | tf_op jit(solution)/shard_map/all_to_all | solution.py:11
  15.1 0.0 copy-done
  15.1 2.9 %copy.44 = f32[4,128,1408]{1,0,2:T(4,128)} copy(f32[4,128,1408]{2,1,0:T(8,128)S(1)} %copy-done) | data formatting | bytes 5767168 | tf_op args[0]
  17.9 0.0 copy-start.4
  17.9 0.0 copy-start.5
  17.9 0.0 copy-start.2
  17.9 4.6 %copy.46 = f32[4,128,1408]{1,0,2:T(4,128)} copy(f32[4,128,1408]{2,1,0:T(8,128)} %param.6) | data formatting | bytes 5767168 | tf_op args[1]
  22.6 0.0 copy-done.4
  22.6 0.0 copy-done.5
  22.6 10.6 %all-to-all-done = f32[16,1,16896]{2,1,0:T(1,128)} async-done(((f32[16,1,16896]{2,1,0:T(1,128)}), f32[16,1,16896]{2,1,0:T(1,128)}, u32[]{:S(2)}, u32[]{:S(2)}) %all-to-all-start) | async-done | bytes 1081376 | tf_op jit(solution)/shard_map/all_to_all | solution.py:11
  33.2 0.6 broadcast_in_dim.5
  33.8 3.5 %all-to-all-start.3 = ((bf16[16,128,4]{1,2,0:T(4,128)(2,1)}), bf16[16,128,4]{1,2,0:T(4,128)(2,1)S(1)}, u32[]{:S(2)}, u32[]{:S(2)}) async-start(bf16[16,128,4]{1,2,0:T(4,128)(2,1)} %broadcast_in_dim.5), calls=%async_computation.3 | async-start | bytes 32768 | tf_op jit(solution)/shard_map/all_to_all | solution.py:11
  37.3 1.9 %reduce_sum.39 = f32[16896]{0:T(1024)S(1)} reduce(f32[16,1,16896]{2,1,0:T(1,128)} %all-to-all-done, f32[]{:T(128)} %constant.6.clone.1), dimensions={0,1}, to_apply=%region_3.0 | reduce | flops 253440 | bytes 1148932 | tf_op jit(solution)/shard_map/reduce_sum | solution.py:15
  39.2 1.2 copy.50
  40.4 0.0 copy-done.2
  40.4 7.7 %fusion = bf16[4,1408,128]{2,0,1:T(4,128)(2,1)} fusion(f32[4,1408,128]{2,1,0:T(8,128)S(1)} %copy-done.2, f32[4,1408]{0,1:T(8,128)} %copy.50), kind=kLoop, calls=%fused_computation.5 | loop fusion | flops 1441792 | bytes 4347904 | tf_op jit(solution)/shard_map/convert_element_type | solution.py:66
  48.1 0.0 copy-start.3
  48.1 1.2 copy.43
  49.3 1.2 copy.45
  50.5 0.0 all-to-all-done.3
  50.5 7.2 %all-to-all-start.2 = ((bf16[4,1408,128]{2,0,1:T(4,128)(2,1)}), bf16[4,1408,128]{2,0,1:T(4,128)(2,1)}, u32[]{:S(2)}, u32[]{:S(2)}) async-start(bf16[4,1408,128]{2,0,1:T(4,128)(2,1)} %fusion), calls=%async_computation.2 | async-start | bytes 2883584 | tf_op jit(solution)/shard_map/all_to_all | solution.py:69
  57.7 0.0 copy-done.3
  57.7 6.6 %divide_convert_fusion = (bf16[4,128,1408]{1,0,2:T(4,128)(2,1)S(1)}, bf16[4,128,1408]{1,0,2:T(4,128)(2,1)S(1)}) fusion(f32[4,128,1408]{1,0,2:T(4,128)} %copy.46, f32[4,1408]{0,1:T(8,128)} %copy.45, f32[4,128,1408]{1,0,2:T(4,128)S(1)} %copy-done.3, f32[4,1408]{0,1:T(8,128)} %copy.43), kind=kLoop, calls=%fused_computation.6 | loop fusion | flops 2883584 | bytes 8695808 | tf_op jit(solution)/shard_map/convert_element_type | solution.py:65
  64.2 2.6 %pad_maximum_fusion = bf16[8,128,1408]{1,0,2:T(8,128)(2,1)} fusion(bf16[4,128,1408]{1,0,2:T(4,128)(2,1)S(1)} %get-tuple-element.12, bf16[4,128,1408]{1,0,2:T(4,128)(2,1)S(1)} %get-tuple-element.13), kind=kLoop, calls=%fused_computation | loop fusion | flops 5767168 | bytes 5767168 | tf_op jit(solution)/shard_map/concatenate | solution.py:28
  66.9 12.0 %all-to-all-done.2 = bf16[4,1408,128]{2,0,1:T(4,128)(2,1)} async-done(((bf16[4,1408,128]{2,0,1:T(4,128)(2,1)}), bf16[4,1408,128]{2,0,1:T(4,128)(2,1)}, u32[]{:S(2)}, u32[]{:S(2)}) %all-to-all-start.2) | async-done | bytes 1441824 | tf_op jit(solution)/shard_map/all_to_all | solution.py:69
  78.8 3.7 %all-to-all-start.1 = ((bf16[8,128,1408]{1,0,2:T(8,128)(2,1)}), bf16[8,128,1408]{1,0,2:T(8,128)(2,1)S(1)}, u32[]{:S(2)}, u32[]{:S(2)}) async-start(bf16[8,128,1408]{1,0,2:T(8,128)(2,1)} %pad_maximum_fusion), calls=%async_computation.1 | async-start | bytes 5767168 | tf_op jit(solution)/shard_map/all_to_all | solution.py:30
  82.6 14.6 %all-gather = bf16[16,4,2048]{2,1,0:T(4,128)(2,1)S(1)} all-gather(bf16[1,4,2048]{2,1,0:T(4,128)(2,1)S(1)} %bitcast.28), channel_id=1, replica_groups=mesh['bank'=16,'zero'=16] {'bank'}, dimensions={0}, use_global_device_ids=true | all-gather | bytes 278528 | tf_op jit(solution)/shard_map/all_gather | solution.py:81
  97.2 0.8 reshape.77
  98.0 0.6 constant_dynamic-slice_fusion.2
  98.6 0.7 constant_dynamic-slice_fusion
  99.3 3.0 %copy.52 = bf16[4,88,16,128]{3,2,1,0:T(8,128)(2,1)} copy(bf16[4,88,16,128]{3,0,1,2:T(4,128)(2,1)} %bitcast.4) | data formatting | bytes 2883584 | tf_op jit(solution)/shard_map/all_to_all | solution.py:69
  102.3 3.5 %all_to_all.38 = bf16[4,88,2048]{2,1,0:T(8,128)(2,1)} reshape(bf16[4,88,16,128]{3,2,1,0:T(8,128)(2,1)} %copy.52) | data formatting | bytes 2883584 | tf_op jit(solution)/shard_map/all_to_all | solution.py:69
  105.8 16.3 %all-to-all-done.1 = bf16[8,128,1408]{1,0,2:T(8,128)(2,1)S(1)} async-done(((bf16[8,128,1408]{1,0,2:T(8,128)(2,1)}), bf16[8,128,1408]{1,0,2:T(8,128)(2,1)S(1)}, u32[]{:S(2)}, u32[]{:S(2)}) %all-to-all-start.1) | async-done | bytes 2883616 | tf_op jit(solution)/shard_map/all_to_all | solution.py:30
  122.0 0.4 copy.47
  122.4 0.2 slice_bitcast_fusion
  122.6 1.5 %copy.64 = bf16[4,16,11,8,128]{4,3,1,2,0:T(8,128)(2,1)} copy(bf16[4,16,11,8,128]{4,3,2,1,0:T(8,128)(2,1)S(1)} %get-tuple-element.7) | data formatting | bytes 2883584 | tf_op jit(solution)/shard_map/slice | solution.py:35
  124.1 1.5 %copy.65 = bf16[4,16,11,8,128]{4,3,1,2,0:T(8,128)(2,1)} copy(bf16[4,16,11,8,128]{4,3,2,1,0:T(8,128)(2,1)S(1)} %get-tuple-element.8) | data formatting | bytes 2883584 | tf_op jit(solution)/shard_map/slice | solution.py:35
  (9 shorter events, 0.1 us)
Async XLA Ops:
  0.6 2.7 %copy-start.1 = (f32[4,128,1408]{2,1,0:T(8,128)S(1)}, f32[4,128,1408]{2,1,0:T(8,128)}, u32[]{:S(2)}) copy-start(f32[4,128,1408]{2,1,0:T(8,128)} %param.6) | copy-start | bytes 8650756
  3.6 11.5 %copy-start = (f32[4,128,1408]{2,1,0:T(8,128)S(1)}, f32[4,128,1408]{2,1,0:T(8,128)}, u32[]{:S(2)}) copy-start(f32[4,128,1408]{2,1,0:T(8,128)} %param.5) | copy-start | bytes 8650756
  8.0 25.2 %all-to-all-start = ((f32[16,1,16896]{2,1,0:T(1,128)}), f32[16,1,16896]{2,1,0:T(1,128)}, u32[]{:S(2)}, u32[]{:S(2)}) async-start(f32[16,1,16896]{2,1,0:T(1,128)} %broadcast_in_dim.4), calls=%async_computation | async-start | bytes 2162688 | tf_op jit(solution)/shard_map/all_to_all | solution.py:11
  17.9 4.7 %copy-start.4 = (f32[128,4]{0,1:T(4,128)S(1)}, f32[128,4]{0,1:T(4,128)}, u32[]{:S(2)}) copy-start(f32[128,4]{0,1:T(4,128)} %param.8) | copy-start | bytes 6148
  17.9 4.7 %copy-start.5 = (f32[128]{0:T(128)S(1)}, f32[128]{0:T(128)}, u32[]{:S(2)}) copy-start(f32[128]{0:T(128)} %param.9) | copy-start | bytes 1540
  17.9 22.5 %copy-start.2 = (f32[4,1408,128]{2,1,0:T(8,128)S(1)}, f32[4,1408,128]{2,1,0:T(8,128)}, u32[]{:S(2)}) copy-start(f32[4,1408,128]{2,1,0:T(8,128)} %param.7) | copy-start | bytes 8650756
  33.8 16.7 %all-to-all-start.3 = ((bf16[16,128,4]{1,2,0:T(4,128)(2,1)}), bf16[16,128,4]{1,2,0:T(4,128)(2,1)S(1)}, u32[]{:S(2)}, u32[]{:S(2)}) async-start(bf16[16,128,4]{1,2,0:T(4,128)(2,1)} %broadcast_in_dim.5), calls=%async_computation.3 | async-start | bytes 32768 | tf_op jit(solution)/shard_map/all_to_all | solution.py:11
  48.1 9.6 %copy-start.3 = (f32[4,128,1408]{1,0,2:T(4,128)S(1)}, f32[4,128,1408]{1,0,2:T(4,128)}, u32[]{:S(2)}) copy-start(f32[4,128,1408]{1,0,2:T(4,128)} %copy.44) | copy-start | bytes 8650756
  50.5 28.4 %all-to-all-start.2 = ((bf16[4,1408,128]{2,0,1:T(4,128)(2,1)}), bf16[4,1408,128]{2,0,1:T(4,128)(2,1)}, u32[]{:S(2)}, u32[]{:S(2)}) async-start(bf16[4,1408,128]{2,0,1:T(4,128)(2,1)} %fusion), calls=%async_computation.2 | async-start | bytes 2883584 | tf_op jit(solution)/shard_map/all_to_all | solution.py:69
  78.8 43.2 %all-to-all-start.1 = ((bf16[8,128,1408]{1,0,2:T(8,128)(2,1)}), bf16[8,128,1408]{1,0,2:T(8,128)(2,1)S(1)}, u32[]{:S(2)}, u32[]{:S(2)}) async-start(bf16[8,128,1408]{1,0,2:T(8,128)(2,1)} %pad_maximum_fusion), calls=%async_computation.1 | async-start | bytes 5767168 | tf_op jit(solution)/shard_map/all_to_all | solution.py:30
where the time goes:
time: 126 us
  waiting for transfers between devices  38.8 us (31%)
  local copies, waits for them, and re-layouts  25.8 us (20%)
  other arithmetic  24.1 us (19%)
  starting transfers between devices  21.5 us (17%)
  blocking collectives  14.6 us (12%)
    all_to_all x1, waiting for transfers between devices, side_by_side(): lax.all_to_all(both, axis, split_axis=split_dim, concat_axis=concat_dim,...  16.3 us
    all_gather x1, blocking collectives, local(): serve_router = lax.all_gather(row_router, 'bank', axis=1, tiled=True)  14.6 us
    all_to_all x1, waiting for transfers between devices, local(): lax.all_to_all(narrow_down, 'zero', split_axis=1, concat_axis=2, tiled=True)  12 us
    all_to_all x2, waiting for transfers between devices, copy_for_each(): lax.all_to_all(jnp.broadcast_to(x[None], (count, *x.shape)), axis, 0, 0,...  10.6 us
    all_to_all x2, starting transfers between devices, copy_for_each(): lax.all_to_all(jnp.broadcast_to(x[None], (count, *x.shape)), axis, 0, 0,...  10.6 us
    unnamed x16, local copies, waits for them, and re-layouts  8.94 us
    convert_element_type x1, other arithmetic, local(): (master_down / jnp.expand_dims(scale_down, 2)).astype(jnp.bfloat16)  7.73 us
    all_to_all x1, starting transfers between devices, local(): lax.all_to_all(narrow_down, 'zero', split_axis=1, concat_axis=2, tiled=True)  7.2 us
  transfers between devices with their start and end apart: 4, of which 3 were waited for; matrix products, arithmetic and copies ran while one was open for 28% of the time, Pallas kernels for 0%

commit v1 on v0

--- a/solution.py
+++ b/solution.py
@@ -66,7 +66,12 @@
         (master_down / jnp.expand_dims(scale_down, 2)).astype(jnp.bfloat16),
     )
     final_gate, final_up = side_by_side((narrow_gate, narrow_up), "zero", 2, 1, 0)
-    final_down = lax.all_to_all(narrow_down, "zero", split_axis=1, concat_axis=2, tiled=True)
+    final_down = jnp.concatenate(
+        lax.all_to_all(
+            jnp.stack(jnp.split(narrow_down, lax.axis_size("zero"), axis=1)), "zero", 0, 0
+        ),
+        axis=2,
+    )
     scale_gate = lax.dynamic_slice_in_dim(
         scale_gate, lax.axis_index("zero") * final_gate.shape[2], final_gate.shape[2], axis=1
     )

time: 126 us -> 119 us (0.944)
  other arithmetic: 24.1 us -> 17.1 us
  waiting for transfers between devices: 38.8 us -> 43.5 us
  local copies, waits for them, and re-layouts: 25.8 us -> 21.7 us
    convert_element_type x1, other arithmetic: 7.73 us -> 0.94 us  [local(): (master_down / jnp.expand_dims(scale_down, 2)).astype(jnp.bfloat16)]
    all_to_all x2 -> x0, local copies, waits for them, and re-layouts: 6.5 us -> none  [local(): lax.all_to_all(narrow_down, 'zero', split_axis=1, concat_axis=2, tiled=True)]
    all_to_all x1, waiting for transfers between devices: 16.3 us -> 20.1 us  [side_by_side(): lax.all_to_all(both, axis, split_axis=split_dim, concat_axis=concat_dim,...]
    reshape x0 -> x1, local copies, waits for them, and re-layouts: none -> 2.65 us  [local(): jnp.concatenate(lax.all_to_all(jnp.stack(jnp.split(narrow_down, lax.axis_...]
    unnamed x16 -> x31, local copies, waits for them, and re-layouts: 8.94 us -> 9.83 us
  transfers between devices with their start and end apart: 4 -> 4, of which waited for: 3 -> 4; matrix products, arithmetic and copies ran while one was open for 28% -> 23% of each run, Pallas kernels for 0% -> 0%
where the time goes in v1:
time: 119 us
  waiting for transfers between devices  43.5 us (37%)
  local copies, waits for them, and re-layouts  21.7 us (18%)
  starting transfers between devices  20.9 us (18%)
  other arithmetic  17.1 us (14%)
  blocking collectives  14.6 us (12%)
    all_to_all x1, waiting for transfers between devices, side_by_side(): lax.all_to_all(both, axis, split_axis=split_dim, concat_axis=concat_dim,...  20.1 us
    all_gather x1, blocking collectives, local(): serve_router = lax.all_gather(row_router, 'bank', axis=1, tiled=True)  14.6 us
    all_to_all x1, waiting for transfers between devices, local(): lax.all_to_all(jnp.stack(jnp.split(narrow_down, lax.axis_size('zero'), ax...  12 us
    all_to_all x2, waiting for transfers between devices, copy_for_each(): lax.all_to_all(jnp.broadcast_to(x[None], (count, *x.shape)), axis, 0, 0,...  11.4 us
    all_to_all x2, starting transfers between devices, copy_for_each(): lax.all_to_all(jnp.broadcast_to(x[None], (count, *x.shape)), axis, 0, 0,...  10.6 us
    unnamed x31, local copies, waits for them, and re-layouts  9.83 us
    all_to_all x1, starting transfers between devices, local(): lax.all_to_all(jnp.stack(jnp.split(narrow_down, lax.axis_size('zero'), ax...  6.64 us
    convert_element_type x1, other arithmetic, local(): (master_up / jnp.expand_dims(scale_up, 1)).astype(jnp.bfloat16)  6.53 us
  transfers between devices with their start and end apart: 4, of which 4 were waited for; matrix products, arithmetic and copies ran while one was open for 23% of the time, Pallas kernels for 0%

profile of v1, /device:TPU:224, one launch (start us, length us, event | category | flops | bytes accessed | tf_op | source)
XLA Modules:
  0.0 118.8 jit_solution(10859366820863062998)
XLA Ops:
  0.6 0.0 copy-start
  0.6 2.8 %abs_reduce_fusion = f32[4,1408]{1,0:T(4,128)S(1)} fusion(f32[4,1408,128]{2,1,0:T(8,128)} %param.7), kind=kLoop, calls=%fused_computation.2 | loop fusion | flops 1436160 | bytes 2906112 | tf_op jit(solution)/shard_map/reduce_sum | solution.py:56
  3.5 0.0 copy-done
  3.5 0.2 abs_reduce_fusion.1
  3.7 2.1 %abs_reduce_fusion.2 = f32[4,1408]{1,0:T(4,128)S(1)} fusion(f32[4,128,1408]{2,1,0:T(8,128)} %param.5), kind=kLoop, calls=%fused_computation.4 | loop fusion | flops 1436160 | bytes 2906112 | tf_op jit(solution)/shard_map/reduce_sum | solution.py:54
  5.8 1.5 %broadcast_in_dim.4 = f32[16,1,16896]{2,1,0:T(1,128)} broadcast(f32[16896]{0:T(1024)S(1)} %pad_maximum_fusion.1), dimensions={2} | broadcast | bytes 1148928 | tf_op jit(solution)/shard_map/broadcast_in_dim | solution.py:11
  7.4 7.1 %all-to-all-start = ((f32[16,1,16896]{2,1,0:T(1,128)}), f32[16,1,16896]{2,1,0:T(1,128)}, u32[]{:S(2)}, u32[]{:S(2)}) async-start(f32[16,1,16896]{2,1,0:T(1,128)} %broadcast_in_dim.4), calls=%async_computation | async-start | bytes 2162688 | tf_op jit(solution)/shard_map/all_to_all | solution.py:11
  14.5 2.8 %copy.42 = f32[4,128,1408]{1,0,2:T(4,128)} copy(f32[4,128,1408]{2,1,0:T(8,128)S(1)} %copy-done) | data formatting | bytes 5767168 | tf_op args[1]
  17.3 0.0 copy-start.4
  17.3 0.0 copy-start.5
  17.3 0.0 copy-start.1
  17.3 4.7 %copy.40 = f32[4,128,1408]{1,0,2:T(4,128)} copy(f32[4,128,1408]{2,1,0:T(8,128)} %param.5) | data formatting | bytes 5767168 | tf_op args[0]
  22.0 0.0 copy-done.4
  22.0 0.0 copy-done.5
  22.0 10.6 %all-to-all-done = f32[16,1,16896]{2,1,0:T(1,128)} async-done(((f32[16,1,16896]{2,1,0:T(1,128)}), f32[16,1,16896]{2,1,0:T(1,128)}, u32[]{:S(2)}, u32[]{:S(2)}) %all-to-all-start) | async-done | bytes 1081376 | tf_op jit(solution)/shard_map/all_to_all | solution.py:11
  32.6 0.6 broadcast_in_dim.5
  33.2 3.5 %all-to-all-start.3 = ((bf16[16,128,4]{1,2,0:T(4,128)(2,1)}), bf16[16,128,4]{1,2,0:T(4,128)(2,1)S(1)}, u32[]{:S(2)}, u32[]{:S(2)}) async-start(bf16[16,128,4]{1,2,0:T(4,128)(2,1)} %broadcast_in_dim.5), calls=%async_computation.3 | async-start | bytes 32768 | tf_op jit(solution)/shard_map/all_to_all | solution.py:11
  36.7 1.9 %reduce_sum.39 = f32[16896]{0:T(1024)S(1)} reduce(f32[16,1,16896]{2,1,0:T(1,128)} %all-to-all-done, f32[]{:T(128)} %constant.6.clone.1), dimensions={0,1}, to_apply=%region_3.0 | reduce | flops 253440 | bytes 1148932 | tf_op jit(solution)/shard_map/reduce_sum | solution.py:15
  38.6 0.0 copy-done.1
  38.7 0.9 divide_convert_fusion
  40.0 0.0 copy-start.3
  40.0 1.1 copy-done.3
  41.1 1.2 copy.41
  42.2 1.2 copy.39
  43.4 0.0 copy-start.2
  43.4 0.8 all-to-all-done.3
  44.2 6.6 %all-to-all-start.2 = ((bf16[16,4,88,128]{3,2,1,0:T(8,128)(2,1)}), bf16[16,4,88,128]{3,2,1,0:T(8,128)(2,1)}, u32[]{:S(2)}, u32[]{:S(2)}) async-start(bf16[16,4,88,128]{3,2,1,0:T(8,128)(2,1)} %copy-done.3), calls=%async_computation.2 | async-start | bytes 2883584 | tf_op jit(solution)/shard_map/all_to_all | solution.py:70
  50.9 0.0 copy-done.2
  50.9 6.5 %divide_convert_fusion.1 = (bf16[4,128,1408]{1,0,2:T(4,128)(2,1)S(1)}, bf16[4,128,1408]{1,0,2:T(4,128)(2,1)S(1)}) fusion(f32[4,128,1408]{1,0,2:T(4,128)S(1)} %copy-done.2, f32[4,1408]{0,1:T(8,128)} %copy.41, f32[4,128,1408]{1,0,2:T(4,128)} %copy.40, f32[4,1408]{0,1:T(8,128)} %copy.39), kind=kLoop, calls=%fused_computation.5 | loop fusion | flops 2883584 | bytes 8695808 | tf_op jit(solution)/shard_map/convert_element_type | solution.py:65
  57.4 2.6 %pad_maximum_fusion = bf16[8,128,1408]{1,0,2:T(8,128)(2,1)} fusion(bf16[4,128,1408]{1,0,2:T(4,128)(2,1)S(1)} %get-tuple-element.12, bf16[4,128,1408]{1,0,2:T(4,128)(2,1)S(1)} %get-tuple-element.13), kind=kLoop, calls=%fused_computation | loop fusion | flops 5767168 | bytes 5767168 | tf_op jit(solution)/shard_map/concatenate | solution.py:28
  60.0 12.0 %all-to-all-done.2 = bf16[16,4,88,128]{3,2,1,0:T(8,128)(2,1)} async-done(((bf16[16,4,88,128]{3,2,1,0:T(8,128)(2,1)}), bf16[16,4,88,128]{3,2,1,0:T(8,128)(2,1)}, u32[]{:S(2)}, u32[]{:S(2)}) %all-to-all-start.2) | async-done | bytes 1441824 | tf_op jit(solution)/shard_map/all_to_all | solution.py:70
  72.0 3.7 %all-to-all-start.1 = ((bf16[8,128,1408]{1,0,2:T(8,128)(2,1)}), bf16[8,128,1408]{1,0,2:T(8,128)(2,1)S(1)}, u32[]{:S(2)}, u32[]{:S(2)}) async-start(bf16[8,128,1408]{1,0,2:T(8,128)(2,1)} %pad_maximum_fusion), calls=%async_computation.1 | async-start | bytes 5767168 | tf_op jit(solution)/shard_map/all_to_all | solution.py:30
  75.8 14.6 %all-gather = bf16[16,4,2048]{2,1,0:T(4,128)(2,1)S(1)} all-gather(bf16[1,4,2048]{2,1,0:T(4,128)(2,1)S(1)} %bitcast.93), channel_id=1, replica_groups=mesh['bank'=16,'zero'=16] {'bank'}, dimensions={0}, use_global_device_ids=true | all-gather | bytes 278528 | tf_op jit(solution)/shard_map/all_gather | solution.py:86
  90.4 0.8 reshape.85
  91.2 0.6 constant_dynamic-slice_fusion.2
  91.8 0.7 constant_dynamic-slice_fusion
  92.5 2.6 %copy_bitcast_fusion = bf16[4,88,2048]{2,1,0:T(8,128)(2,1)} fusion(bf16[16,4,88,128]{3,2,1,0:T(8,128)(2,1)} %all-to-all-done.2), kind=kLoop, calls=%fused_computation.7 | loop fusion | bytes 2883584 | tf_op jit(solution)/shard_map/reshape | solution.py:69
  95.1 20.1 %all-to-all-done.1 = bf16[8,128,1408]{1,0,2:T(8,128)(2,1)S(1)} async-done(((bf16[8,128,1408]{1,0,2:T(8,128)(2,1)}), bf16[8,128,1408]{1,0,2:T(8,128)(2,1)S(1)}, u32[]{:S(2)}, u32[]{:S(2)}) %all-to-all-start.1) | async-done | bytes 2883616 | tf_op jit(solution)/shard_map/all_to_all | solution.py:30
  115.2 0.4 copy.43
  115.6 0.2 slice_bitcast_fusion
  115.8 1.5 %copy.58 = bf16[4,16,11,8,128]{4,3,1,2,0:T(8,128)(2,1)} copy(bf16[4,16,11,8,128]{4,3,2,1,0:T(8,128)(2,1)S(1)} %get-tuple-element.8) | data formatting | bytes 2883584 | tf_op jit(solution)/shard_map/slice | solution.py:35
  117.3 1.5 %copy.57 = bf16[4,16,11,8,128]{4,3,1,2,0:T(8,128)(2,1)} copy(bf16[4,16,11,8,128]{4,3,2,1,0:T(8,128)(2,1)S(1)} %get-tuple-element.7) | data formatting | bytes 2883584 | tf_op jit(solution)/shard_map/slice | solution.py:35
  (25 shorter events, 0.4 us)
Async XLA Ops:
  0.6 2.8 %copy-start = (f32[4,128,1408]{2,1,0:T(8,128)S(1)}, f32[4,128,1408]{2,1,0:T(8,128)}, u32[]{:S(2)}) copy-start(f32[4,128,1408]{2,1,0:T(8,128)} %param.6) | copy-start | bytes 8650756
  7.4 25.2 %all-to-all-start = ((f32[16,1,16896]{2,1,0:T(1,128)}), f32[16,1,16896]{2,1,0:T(1,128)}, u32[]{:S(2)}, u32[]{:S(2)}) async-start(f32[16,1,16896]{2,1,0:T(1,128)} %broadcast_in_dim.4), calls=%async_computation | async-start | bytes 2162688 | tf_op jit(solution)/shard_map/all_to_all | solution.py:11
  17.3 4.7 %copy-start.4 = (f32[128,4]{0,1:T(4,128)S(1)}, f32[128,4]{0,1:T(4,128)}, u32[]{:S(2)}) copy-start(f32[128,4]{0,1:T(4,128)} %param.8) | copy-start | bytes 6148
  17.3 4.7 %copy-start.5 = (f32[128]{0:T(128)S(1)}, f32[128]{0:T(128)}, u32[]{:S(2)}) copy-start(f32[128]{0:T(128)} %param.9) | copy-start | bytes 1540
  17.3 21.3 %copy-start.1 = (f32[4,1408,128]{2,1,0:T(8,128)S(1)}, f32[4,1408,128]{2,1,0:T(8,128)}, u32[]{:S(2)}) copy-start(f32[4,1408,128]{2,1,0:T(8,128)} %param.7) | copy-start | bytes 8650756
  33.2 11.0 %all-to-all-start.3 = ((bf16[16,128,4]{1,2,0:T(4,128)(2,1)}), bf16[16,128,4]{1,2,0:T(4,128)(2,1)S(1)}, u32[]{:S(2)}, u32[]{:S(2)}) async-start(bf16[16,128,4]{1,2,0:T(4,128)(2,1)} %broadcast_in_dim.5), calls=%async_computation.3 | async-start | bytes 32768 | tf_op jit(solution)/shard_map/all_to_all | solution.py:11
  40.0 1.1 copy-start.3
  43.4 7.5 %copy-start.2 = (f32[4,128,1408]{1,0,2:T(4,128)S(1)}, f32[4,128,1408]{1,0,2:T(4,128)}, u32[]{:S(2)}) copy-start(f32[4,128,1408]{1,0,2:T(4,128)} %copy.42) | copy-start | bytes 8650756
  44.2 27.8 %all-to-all-start.2 = ((bf16[16,4,88,128]{3,2,1,0:T(8,128)(2,1)}), bf16[16,4,88,128]{3,2,1,0:T(8,128)(2,1)}, u32[]{:S(2)}, u32[]{:S(2)}) async-start(bf16[16,4,88,128]{3,2,1,0:T(8,128)(2,1)} %copy-done.3), calls=%async_computation.2 | async-start | bytes 2883584 | tf_op jit(solution)/shard_map/all_to_all | solution.py:70
  72.0 43.2 %all-to-all-start.1 = ((bf16[8,128,1408]{1,0,2:T(8,128)(2,1)}), bf16[8,128,1408]{1,0,2:T(8,128)(2,1)S(1)}, u32[]{:S(2)}, u32[]{:S(2)}) async-start(bf16[8,128,1408]{1,0,2:T(8,128)(2,1)} %pad_maximum_fusion), calls=%async_computation.1 | async-start | bytes 5767168 | tf_op jit(solution)/shard_map/all_to_all | solution.py:30
